TPU v7x, 256 devices: a whole 4x4x8 slice. The times are simulated.
256 devices in a mesh: vtx: 64 (over z, y_lo, x), src: 4 (over y_hi, core).
Axes of the slice: x: 4, y: 4 (y_hi: 2, y_lo: 2; y = y_hi * 2 + y_lo), z: 8, core: 2. Of those that a mesh axis runs over, the one named last changes fastest.
Arguments:
- heat: float32 [64, 512, 8192], P(None, ('vtx', 'src')), may hold values from -12 to 12
- cotan: float32 [4, 512, 8192], P(None, 'vtx'), may hold values from 0.2 to 2
- source_index: int32 [64], replicated, may hold values from 0 to 4194303
Outputs:
- normalised: float32 [64, 512, 8192], P('src', 'vtx')
- col_norm: float32 [64], P('src')
Inputs may be any that keep to these rules, and one draw needn't show every extreme that they name: `source_index`: row-major vertex indices, sources may share a vertex.
All inputs are finite; a program needn't handle non-finite values.
Results may differ from a plain program's by a relative error of at most 0.0003.
Values sent between devices are 32-bit elements; how exact they have to be, the bound alone decides.
A program may use at most 64 MiB of HBM per device.

v0:
```python
import math
import jax
import jax.numpy as jnp
from jax import lax
from jax.sharding import PartitionSpec as P


def from_behind(value, axis, by):
    peers = lax.axis_size(axis)
    pairs = [(i, i + by) for i in range(peers) if 0 <= i + by < peers]
    return lax.ppermute(value, axis, pairs)


def extended(value, sides, width):
    for axis, dim in sides:
        peers, length = (lax.axis_size(axis), value.shape[dim])
        up = [(i, (i + 1) % peers) for i in range(peers - 1)]
        down = [(j, i) for i, j in up]
        last = lax.slice_in_dim(value, length - width, length, axis=dim)
        first = lax.slice_in_dim(value, 0, width, axis=dim)
        before = lax.ppermute(last, axis, up)
        after = lax.ppermute(first, axis, down)
        value = jnp.concatenate([before, value, after], axis=dim)
    return value


def from_everyone(value, axis):
    peers = lax.axis_size(axis)
    return lax.all_to_all(
        jnp.broadcast_to(value[None], (peers, *value.shape)), axis, 0, 0, tiled=True
    )


def taken_together(value, axis):
    everything = from_everyone(value, axis)
    return jnp.sum(everything, axis=0)


def from_right(values):
    return jnp.concatenate([values[..., 1:], jnp.zeros_like(values[..., :1])], axis=-1)


def from_left(values):
    return jnp.concatenate([jnp.zeros_like(values[..., :1]), values[..., :-1]], axis=-1)


def masked_cotan(cotan, row_start, total_rows):
    shape = cotan.shape[1:]
    rows = row_start + lax.broadcasted_iota(jnp.int32, shape, 0)
    cols = lax.broadcasted_iota(jnp.int32, shape, 1)
    inside_col = cols < shape[1] - 1
    inside_row = rows < total_rows - 1
    mass = cotan[0]
    east = jnp.where(inside_col, cotan[1], 0.0)
    north = jnp.where(inside_row, cotan[2], 0.0)
    diag = jnp.where(inside_col & inside_row, cotan[3], 0.0)
    return (mass, east, north, diag)


def stencil_defect(padded, mass, east, north_ext, diag_ext, row_start, sources, amplitude):
    center = padded[:, 1:-1, :]
    above = padded[:, 2:, :]
    below = padded[:, :-2, :]
    north = north_ext[1:]
    south_weight = north_ext[:-1]
    diag = diag_ext[1:]
    southwest_weight = from_left(diag_ext[:-1])
    west_weight = from_left(east)
    result = mass * center + east * (center - from_right(center))
    result = result + west_weight * (center - from_left(center))
    result = result + north * (center - above) + south_weight * (center - below)
    result = (
        result
        + diag * (center - from_right(above))
        + southwest_weight * (center - from_left(below))
    )
    count_rows, width = (center.shape[1], center.shape[2])
    row_ids = row_start + lax.broadcasted_iota(jnp.int32, (count_rows, width), 0)
    col_ids = lax.broadcasted_iota(jnp.int32, (count_rows, width), 1)
    flat = row_ids * width + col_ids
    delta = (flat[None, :, :] == sources[:, None, None]).astype(jnp.float32)
    return result - amplitude * delta


def on_device(heat, cotan, source_index):
    vtx_index = lax.axis_index("vtx")
    rows_dev = cotan.shape[1]
    width = cotan.shape[2]
    total_rows = rows_dev * lax.axis_size("vtx")
    amplitude = math.sqrt(total_rows * width) / 8.0
    block_start = vtx_index * rows_dev
    mass, east, north, diag = masked_cotan(cotan, block_start, total_rows)
    lower = from_behind(jnp.stack([north[-1:], diag[-1:]]), "vtx", 1)
    north_ext = jnp.concatenate([lower[0], north], axis=0)
    diag_ext = jnp.concatenate([lower[1], diag], axis=0)
    src_index = lax.axis_index("src")
    per_group = heat.shape[0] // lax.axis_size("src")
    tile = lax.all_to_all(heat, "src", split_axis=0, concat_axis=1, tiled=True)
    padded = extended(tile, (("vtx", 1),), 1)
    sources = lax.dynamic_slice_in_dim(source_index, src_index * per_group, per_group)
    defect = stencil_defect(
        padded, mass, east, north_ext, diag_ext, block_start, sources, amplitude
    )
    total = taken_together(jnp.sum(defect * defect, axis=(1, 2)), "vtx")
    norms = jnp.sqrt(total / (total_rows * width) + 1e-06)
    return (defect / norms[:, None, None], norms)


def solution(mesh):
    return jax.shard_map(
        on_device,
        mesh=mesh,
        in_specs=(P(None, ("vtx", "src"), None), P(None, "vtx", None), P()),
        out_specs=(P("src", "vtx", None), P("src")),
        check_vma=False,
    )
```

profile of v0, /device:TPU:8, one launch (start us, length us, event | category | flops | bytes accessed | tf_op | source)
XLA Modules:
  0.0 118.3 jit_solution(17329714812238578994)
XLA Ops:
  0.6 0.0 copy-start
  0.6 5.0 %all-to-all-start = ((f32[64,2,8192]{2,1,0:T(2,128)}), f32[64,2,8192]{2,1,0:T(2,128)}, u32[]{:S(2)}, u32[]{:S(2)}) async-start(f32[64,2,8192]{2,1,0:T(2,128)} %param.3), calls=%async_computation | async-start | bytes 8388608 | tf_op jit(solution)/shard_map/all_to_all | solution.py:98
  5.6 0.0 copy-start.2
  5.7 0.0 copy-done
  5.7 0.1 bitcast_select_fusion.1
  5.9 0.1 pad_maximum_fusion.1
  5.9 3.4 %collective-permute-start.1 = (f32[2,1,8192]{2,1,0:T(1,128)S(1)}, f32[2,1,8192]{2,1,0:T(1,128)S(1)}, u32[]{:S(2)}, u32[]{:S(2)}) collective-permute-start(f32[2,1,8192]{2,1,0:T(1,128)S(1)} %pad_maximum_fusion.1), channel_id=1, source_target_pairs={{0,4},{4,8},{8,12},{12,16},{16,20},{20,24},{24,28},{28,32},{32,36}... | collective-permute-start | bytes 196616 | tf_op jit(solution)/shard_map/ppermute | solution.py:11
  9.4 0.1 slice_bitcast_fusion
  9.5 0.1 iota_add_fusion
  9.6 0.0 copy-done.2
  9.6 0.1 dynamic_slice.3
  9.7 0.1 concatenate.32
  9.8 4.6 %collective-permute-done.1 = f32[2,1,8192]{2,1,0:T(1,128)S(1)} collective-permute-done((f32[2,1,8192]{2,1,0:T(1,128)S(1)}, f32[2,1,8192]{2,1,0:T(1,128)S(1)}, u32[]{:S(2)}, u32[]{:S(2)}) %collective-permute-start.1) | collective-permute-done | bytes 65568 | tf_op jit(solution)/shard_map/ppermute | solution.py:11
  14.5 0.2 select_maximum_fusion.2
  14.7 40.6 %all-to-all-done = f32[64,2,8192]{2,1,0:T(2,128)} async-done(((f32[64,2,8192]{2,1,0:T(2,128)}), f32[64,2,8192]{2,1,0:T(2,128)}, u32[]{:S(2)}, u32[]{:S(2)}) %all-to-all-start) | async-done | bytes 4194336 | tf_op jit(solution)/shard_map/all_to_all | solution.py:98
  55.3 4.6 %copy.10 = f32[4,16,2,8192]{3,1,2,0:T(8,128)S(1)} copy(f32[4,16,2,8192]{3,2,1,0:T(2,128)} %bitcast.1) | data formatting | bytes 8388608 | tf_op jit(solution)/shard_map/all_to_all | solution.py:98
  60.0 0.1 fusion.19
  60.0 4.6 %collective-permute-start = (f32[16,1,8192]{2,0,1:T(8,128)S(1)}, f32[16,1,8192]{2,0,1:T(8,128)S(1)}, u32[]{:S(2)}, u32[]{:S(2)}) collective-permute-start(f32[16,1,8192]{2,0,1:T(8,128)S(1)} %get-tuple-element.12), channel_id=1, source_target_pairs={{4,0},{8,4},{12,8},{16,12},{20,16},{24,20},{28,24},{32,28},{36,32}... | collective-permute-start | bytes 1572872 | tf_op jit(solution)/shard_map/ppermute | solution.py:22
  64.6 1.9 %collective-permute-start.2 = (f32[16,1,8192]{2,0,1:T(8,128)S(1)}, f32[16,1,8192]{2,0,1:T(8,128)S(1)}, u32[]{:S(2)}, u32[]{:S(2)}) collective-permute-start(f32[16,1,8192]{2,0,1:T(8,128)S(1)} %get-tuple-element.13), channel_id=1, source_target_pairs={{0,4},{4,8},{8,12},{12,16},{16,20},{20,24},{24,28},{28,32},{32,36}... | collective-permute-start | bytes 1572872 | tf_op jit(solution)/shard_map/ppermute | solution.py:21
  66.5 1.5 %fusion.18 = (f32[16,8,8191]{2,0,1:T(8,128)S(1)}, f32[16,8,8191]{2,0,1:T(8,128)S(1)}) fusion(f32[16,8,8192]{2,0,1:T(8,128)S(1)} %bitcast.28), kind=kLoop, calls=%fused_computation.47 | loop fusion | bytes 16775168 | tf_op jit(solution)/shard_map/slice | solution.py:40
  68.0 7.5 %collective-permute-done = f32[16,1,8192]{2,0,1:T(8,128)S(1)} collective-permute-done((f32[16,1,8192]{2,0,1:T(8,128)S(1)}, f32[16,1,8192]{2,0,1:T(8,128)S(1)}, u32[]{:S(2)}, u32[]{:S(2)}) %collective-permute-start) | collective-permute-done | bytes 524320 | tf_op jit(solution)/shard_map/ppermute | solution.py:22
  75.5 6.2 %collective-permute-done.2 = f32[16,1,8192]{2,0,1:T(8,128)S(1)} collective-permute-done((f32[16,1,8192]{2,0,1:T(8,128)S(1)}, f32[16,1,8192]{2,0,1:T(8,128)S(1)}, u32[]{:S(2)}, u32[]{:S(2)}) %collective-permute-start.2) | collective-permute-done | bytes 524320 | tf_op jit(solution)/shard_map/ppermute | solution.py:21
  81.7 7.7 %multiply_reduce_fusion = (f32[16]{0:T(128)S(1)}, f32[16,8,8192]{2,0,1:T(8,128)}) fusion(s32[16]{0:T(128)S(1)} %dynamic_slice.3, s32[8,8192]{1,0:T(8,128)S(1)} %iota_add_fusion, f32[16,8,8192]{2,0,1:T(8,128)S(1)} %bitcast.29, f32[16,1,8192]{2,0,1:T(8,128)S(1)} %collective-permute-done.2, f32[8,8192]{1,0:T(8,128)S(1)} %get-tuple-element.26, ...), kind=kLoop, calls=%fused_computation.23 | loop fusion | flops 35651568 | bytes 19922048 | tf_op jit(solution)/shard_map/reduce_sum | solution.py:104
  89.4 21.6 %all_to_all.24 = f32[64,1,16]{2,1,0:T(1,128)S(1)} all-to-all(f32[64,1,16]{2,1,0:T(1,128)S(1)} %broadcast_in_dim.12), channel_id=1, replica_groups=mesh['vtx'=64,'src'=4] {'vtx'}, dimensions={0} | all-to-all | bytes 8192 | tf_op jit(solution)/shard_map/all_to_all | solution.py:29
  111.0 0.1 reduce_sum.19
  111.1 0.0 copy-start.1
  111.1 2.7 %broadcast_divide_fusion = f32[16,8,8192]{2,0,1:T(8,128)S(1)} fusion(f32[16,8,8192]{2,0,1:T(8,128)} %get-tuple-element.9, f32[16]{0:T(128)S(1)} %add_sqrt_fusion), kind=kLoop, calls=%fused_computation.24 | loop fusion | flops 1048576 | bytes 8388672 | tf_op jit(solution)/shard_map/div | solution.py:106
  113.9 0.0 copy-done.1
  113.9 4.4 %copy.12 = f32[16,8,8192]{2,1,0:T(8,128)} copy(f32[16,8,8192]{2,0,1:T(8,128)S(1)} %broadcast_divide_fusion) | data formatting | bytes 8388608
  (9 shorter events, 0.2 us)
Async XLA Ops:
  0.6 5.0 %copy-start = (f32[4,8,8192]{2,1,0:T(8,128)S(1)}, f32[4,8,8192]{2,1,0:T(8,128)}, u32[]{:S(2)}) copy-start(f32[4,8,8192]{2,1,0:T(8,128)} %param.4) | copy-start | bytes 3145732
  0.6 54.7 %all-to-all-start = ((f32[64,2,8192]{2,1,0:T(2,128)}), f32[64,2,8192]{2,1,0:T(2,128)}, u32[]{:S(2)}, u32[]{:S(2)}) async-start(f32[64,2,8192]{2,1,0:T(2,128)} %param.3), calls=%async_computation | async-start | bytes 8388608 | tf_op jit(solution)/shard_map/all_to_all | solution.py:98
  5.6 4.0 %copy-start.2 = (s32[64]{0:T(128)S(1)}, s32[64]{0:T(128)}, u32[]{:S(2)}) copy-start(s32[64]{0:T(128)} %param.5) | copy-start | bytes 772
  5.9 8.5 %collective-permute-start.1 = (f32[2,1,8192]{2,1,0:T(1,128)S(1)}, f32[2,1,8192]{2,1,0:T(1,128)S(1)}, u32[]{:S(2)}, u32[]{:S(2)}) collective-permute-start(f32[2,1,8192]{2,1,0:T(1,128)S(1)} %pad_maximum_fusion.1), channel_id=1, source_target_pairs={{0,4},{4,8},{8,12},{12,16},{16,20},{20,24},{24,28},{28,32},{32,36}... | collective-permute-start | bytes 196616 | tf_op jit(solution)/shard_map/ppermute | solution.py:11
  60.0 15.4 %collective-permute-start = (f32[16,1,8192]{2,0,1:T(8,128)S(1)}, f32[16,1,8192]{2,0,1:T(8,128)S(1)}, u32[]{:S(2)}, u32[]{:S(2)}) collective-permute-start(f32[16,1,8192]{2,0,1:T(8,128)S(1)} %get-tuple-element.12), channel_id=1, source_target_pairs={{4,0},{8,4},{12,8},{16,12},{20,16},{24,20},{28,24},{32,28},{36,32}... | collective-permute-start | bytes 1572872 | tf_op jit(solution)/shard_map/ppermute | solution.py:22
  64.6 17.1 %collective-permute-start.2 = (f32[16,1,8192]{2,0,1:T(8,128)S(1)}, f32[16,1,8192]{2,0,1:T(8,128)S(1)}, u32[]{:S(2)}, u32[]{:S(2)}) collective-permute-start(f32[16,1,8192]{2,0,1:T(8,128)S(1)} %get-tuple-element.13), channel_id=1, source_target_pairs={{0,4},{4,8},{8,12},{12,16},{16,20},{20,24},{24,28},{28,32},{32,36}... | collective-permute-start | bytes 1572872 | tf_op jit(solution)/shard_map/ppermute | solution.py:21
  111.1 2.7 %copy-start.1 = (f32[16]{0:T(128)}, f32[16]{0:T(128)S(1)}, u32[]{:S(2)}) copy-start(f32[16]{0:T(128)S(1)} %add_sqrt_fusion) | copy-start | bytes 196
where the time goes:
time: 119 us; the launch traced here: 118 us
  waiting for transfers between devices  59 us (50%)
  blocking collectives  21.6 us (18%)
  starting transfers between devices  14.8 us (12%)
  other arithmetic  11.2 us (9%)
  local copies, waits for them, and re-layouts  10.9 us (9%)
    all_to_all x1, waiting for transfers between devices, on_device(): tile = lax.all_to_all(heat, 'src', split_axis=0, concat_axis=1, tiled=True)  40.6 us
    all_to_all x1, blocking collectives, from_everyone(): lax.all_to_all(jnp.broadcast_to(value[None], (peers, *value.shape)), axis...  21.6 us
    reduce_sum x1, other arithmetic, on_device(): total = taken_together(jnp.sum(defect * defect, axis=(1, 2)), 'vtx')  7.69 us
    ppermute x1, waiting for transfers between devices, extended(): after = lax.ppermute(first, axis, down)  7.47 us
    ppermute x1, waiting for transfers between devices, extended(): before = lax.ppermute(last, axis, up)  6.23 us
    all_to_all x1, starting transfers between devices, on_device(): tile = lax.all_to_all(heat, 'src', split_axis=0, concat_axis=1, tiled=True)  4.97 us
    ppermute x1, waiting for transfers between devices, from_behind(): return lax.ppermute(value, axis, pairs)  4.64 us
    all_to_all x1, local copies, waits for them, and re-layouts, on_device(): tile = lax.all_to_all(heat, 'src', split_axis=0, concat_axis=1, tiled=True)  4.62 us
  transfers between devices with their start and end apart: 4, of which 4 were waited for; matrix products, arithmetic and copies ran while one was open for 2% of the time, Pallas kernels for 0%

commit v1 on v0

--- a/solution.py
+++ b/solution.py
@@ -95,7 +95,11 @@
     diag_ext = jnp.concatenate([lower[1], diag], axis=0)
     src_index = lax.axis_index("src")
     per_group = heat.shape[0] // lax.axis_size("src")
-    tile = lax.all_to_all(heat, "src", split_axis=0, concat_axis=1, tiled=True)
+    res = lax.axis_size("src")
+    arr_next = jnp.split(heat, res, axis=0)
+    known = jnp.stack(arr_next, axis=0)
+    reply = lax.all_to_all(known, axis_name="src", concat_axis=0, split_axis=0)
+    tile = jnp.concatenate(reply, axis=1)
     padded = extended(tile, (("vtx", 1),), 1)
     sources = lax.dynamic_slice_in_dim(source_index, src_index * per_group, per_group)
     defect = stencil_defect(

time: 119 us -> 131 us (1.10)
  other arithmetic: 11.2 us -> 15.8 us
  waiting for transfers between devices: 59 us -> 62.7 us
  local copies, waits for them, and re-layouts: 10.9 us -> 13.6 us
  blocking collectives: 21.6 us -> 23.1 us
    all_to_all x1, waiting for transfers between devices: 40.6 us -> 49 us  [on_device(): reply = lax.all_to_all(known, axis_name='src', concat_axis=0, split_axis=0)]
    ppermute x1, waiting for transfers between devices: 4.64 us -> 0.01 us  [from_behind(): return lax.ppermute(value, axis, pairs)]
    reshape x0 -> x1, local copies, waits for them, and re-layouts: none -> 4.62 us  [on_device(): tile = jnp.concatenate(reply, axis=1)]
    all_to_all x1 -> x0, local copies, waits for them, and re-layouts: 4.62 us -> none  [on_device(): tile = lax.all_to_all(heat, 'src', split_axis=0, concat_axis=1, tiled=True)]
    another operation x0 -> x1, other arithmetic: none -> 3.6 us  [on_device(): known = jnp.stack(arr_next, axis=0)]
    another operation x0 -> x1, local copies, waits for them, and re-layouts: none -> 2.66 us  [on_device(): known = jnp.stack(arr_next, axis=0)]
    all_to_all x1, blocking collectives: 21.6 us -> 23.1 us  [from_everyone(): lax.all_to_all(jnp.broadcast_to(value[None], (peers, *value.shape)), axis...]
  transfers between devices with their start and end apart: 4 -> 4, of which waited for: 4 -> 3; matrix products, arithmetic and copies ran while one was open for 2% -> 6% of each run, Pallas kernels for 0% -> 0%
where the time goes in v1:
time: 131 us
  waiting for transfers between devices  62.7 us (48%)
  blocking collectives  23.1 us (18%)
  other arithmetic  15.8 us (12%)
  starting transfers between devices  14.8 us (11%)
  local copies, waits for them, and re-layouts  13.6 us (10%)
    all_to_all x1, waiting for transfers between devices, on_device(): reply = lax.all_to_all(known, axis_name='src', concat_axis=0, split_axis=0)  49 us
    all_to_all x1, blocking collectives, from_everyone(): lax.all_to_all(jnp.broadcast_to(value[None], (peers, *value.shape)), axis...  23.1 us
    reduce_sum x1, other arithmetic, on_device(): total = taken_together(jnp.sum(defect * defect, axis=(1, 2)), 'vtx')  7.69 us
    ppermute x1, waiting for transfers between devices, extended(): after = lax.ppermute(first, axis, down)  7.47 us
    ppermute x1, waiting for transfers between devices, extended(): before = lax.ppermute(last, axis, up)  6.23 us
    all_to_all x1, starting transfers between devices, on_device(): reply = lax.all_to_all(known, axis_name='src', concat_axis=0, split_axis=0)  4.98 us
    reshape x1, local copies, waits for them, and re-layouts, on_device(): tile = jnp.concatenate(reply, axis=1)  4.62 us
    ppermute x1, starting transfers between devices, extended(): after = lax.ppermute(first, axis, down)  4.55 us
  transfers between devices with their start and end apart: 4, of which 3 were waited for; matrix products, arithmetic and copies ran while one was open for 6% of the time, Pallas kernels for 0%

profile of v1, /device:TPU:8, one launch (start us, length us, event | category | flops | bytes accessed | tf_op | source)
XLA Modules:
  0.0 130.8 jit_solution(152906078681971270)
XLA Ops:
  0.7 1.1 bitcast_select_fusion.1
  1.9 0.1 pad_maximum_fusion.2
  2.0 3.4 %collective-permute-start.1 = (f32[2,1,8192]{2,1,0:T(1,128)S(1)}, f32[2,1,8192]{2,1,0:T(1,128)S(1)}, u32[]{:S(2)}, u32[]{:S(2)}) collective-permute-start(f32[2,1,8192]{2,1,0:T(1,128)S(1)} %pad_maximum_fusion.2), channel_id=1, source_target_pairs={{0,4},{4,8},{8,12},{12,16},{16,20},{20,24},{24,28},{28,32},{32,36}... | collective-permute-start | bytes 196616 | tf_op jit(solution)/shard_map/ppermute | solution.py:11
  5.4 2.7 %slice_bitcast_fusion.3 = (f32[1,16,2,8192]{3,2,1,0:T(2,128)S(1)}, f32[1,16,2,8192]{3,2,1,0:T(2,128)S(1)}, f32[1,16,2,8192]{3,2,1,0:T(2,128)S(1)}, f32[1,16,2,8192]{3,2,1,0:T(2,128)S(1)}) fusion(f32[64,2,8192]{2,1,0:T(2,128)} %param.3), kind=kLoop, calls=%fused_computation.29 | loop fusion | bytes 8388608 | tf_op jit(solution)/shard_map/stack | solution.py:100
  8.0 3.6 %pad_maximum_fusion = f32[4,16,2,8192]{3,2,1,0:T(2,128)} fusion(f32[1,16,2,8192]{3,2,1,0:T(2,128)S(1)} %get-tuple-element.16, f32[1,16,2,8192]{3,2,1,0:T(2,128)S(1)} %get-tuple-element.17, f32[1,16,2,8192]{3,2,1,0:T(2,128)S(1)} %get-tuple-element.15, f32[1,16,2,8192]{3,2,1,0:T(2,128)S(1)} %get-tuple-element.14), kind=kLoop, calls=%fused_computation.23 | loop fusion | flops 3145728 | bytes 8388608 | tf_op jit(solution)/shard_map/stack | solution.py:100
  11.6 0.0 copy-start
  11.6 0.0 copy-start.2
  11.6 5.0 %all-to-all-start = ((f32[4,16,2,8192]{3,2,1,0:T(2,128)}), f32[4,16,2,8192]{3,2,1,0:T(2,128)}, u32[]{:S(2)}, u32[]{:S(2)}) async-start(f32[4,16,2,8192]{3,2,1,0:T(2,128)} %pad_maximum_fusion), calls=%async_computation | async-start | bytes 8388608 | tf_op jit(solution)/shard_map/all_to_all | solution.py:101
  16.6 0.0 copy-done
  16.6 0.1 slice_bitcast_fusion.4
  16.8 0.1 iota_add_fusion
  16.9 0.0 copy-done.2
  16.9 0.1 dynamic_slice.3
  17.0 0.1 concatenate.32
  17.1 0.0 collective-permute-done.1
  17.2 0.2 select_maximum_fusion.2
  17.4 49.0 %all-to-all-done = f32[4,16,2,8192]{3,2,1,0:T(2,128)} async-done(((f32[4,16,2,8192]{3,2,1,0:T(2,128)}), f32[4,16,2,8192]{3,2,1,0:T(2,128)}, u32[]{:S(2)}, u32[]{:S(2)}) %all-to-all-start) | async-done | bytes 4194336 | tf_op jit(solution)/shard_map/all_to_all | solution.py:101
  66.3 4.6 %copy.10 = f32[16,4,2,8192]{3,0,2,1:T(8,128)S(1)} copy(f32[16,4,2,8192]{3,2,0,1:T(2,128)} %bitcast.5) | data formatting | bytes 8388608 | tf_op jit(solution)/shard_map/reshape | solution.py:102
  71.0 0.1 fusion.19
  71.0 4.6 %collective-permute-start = (f32[16,1,8192]{2,0,1:T(8,128)S(1)}, f32[16,1,8192]{2,0,1:T(8,128)S(1)}, u32[]{:S(2)}, u32[]{:S(2)}) collective-permute-start(f32[16,1,8192]{2,0,1:T(8,128)S(1)} %get-tuple-element.12), channel_id=1, source_target_pairs={{4,0},{8,4},{12,8},{16,12},{20,16},{24,20},{28,24},{32,28},{36,32}... | collective-permute-start | bytes 1572872 | tf_op jit(solution)/shard_map/ppermute | solution.py:22
  75.6 1.9 %collective-permute-start.2 = (f32[16,1,8192]{2,0,1:T(8,128)S(1)}, f32[16,1,8192]{2,0,1:T(8,128)S(1)}, u32[]{:S(2)}, u32[]{:S(2)}) collective-permute-start(f32[16,1,8192]{2,0,1:T(8,128)S(1)} %get-tuple-element.13), channel_id=1, source_target_pairs={{0,4},{4,8},{8,12},{12,16},{16,20},{20,24},{24,28},{28,32},{32,36}... | collective-permute-start | bytes 1572872 | tf_op jit(solution)/shard_map/ppermute | solution.py:21
  77.5 1.5 %fusion.18 = (f32[16,8,8191]{2,0,1:T(8,128)S(1)}, f32[16,8,8191]{2,0,1:T(8,128)S(1)}) fusion(f32[16,8,8192]{2,0,1:T(8,128)S(1)} %bitcast.34), kind=kLoop, calls=%fused_computation.52 | loop fusion | bytes 16775168 | tf_op jit(solution)/shard_map/slice | solution.py:40
  79.0 7.5 %collective-permute-done = f32[16,1,8192]{2,0,1:T(8,128)S(1)} collective-permute-done((f32[16,1,8192]{2,0,1:T(8,128)S(1)}, f32[16,1,8192]{2,0,1:T(8,128)S(1)}, u32[]{:S(2)}, u32[]{:S(2)}) %collective-permute-start) | collective-permute-done | bytes 524320 | tf_op jit(solution)/shard_map/ppermute | solution.py:22
  86.5 6.2 %collective-permute-done.2 = f32[16,1,8192]{2,0,1:T(8,128)S(1)} collective-permute-done((f32[16,1,8192]{2,0,1:T(8,128)S(1)}, f32[16,1,8192]{2,0,1:T(8,128)S(1)}, u32[]{:S(2)}, u32[]{:S(2)}) %collective-permute-start.2) | collective-permute-done | bytes 524320 | tf_op jit(solution)/shard_map/ppermute | solution.py:21
  92.7 7.7 %multiply_reduce_fusion = (f32[16]{0:T(128)S(1)}, f32[16,8,8192]{2,0,1:T(8,128)}) fusion(s32[16]{0:T(128)S(1)} %dynamic_slice.3, s32[8,8192]{1,0:T(8,128)S(1)} %iota_add_fusion, f32[16,8,8192]{2,0,1:T(8,128)S(1)} %bitcast.35, f32[16,1,8192]{2,0,1:T(8,128)S(1)} %collective-permute-done.2, f32[8,8192]{1,0:T(8,128)S(1)} %get-tuple-element.30, ...), kind=kLoop, calls=%fused_computation.24 | loop fusion | flops 35651568 | bytes 19922048 | tf_op jit(solution)/shard_map/reduce_sum | solution.py:108
  100.4 23.1 %all_to_all.11 = f32[64,1,16]{2,1,0:T(1,128)S(1)} all-to-all(f32[64,1,16]{2,1,0:T(1,128)S(1)} %broadcast_in_dim.12), channel_id=1, replica_groups=mesh['vtx'=64,'src'=4] {'vtx'}, dimensions={0} | all-to-all | bytes 8192 | tf_op jit(solution)/shard_map/all_to_all | solution.py:29
  123.5 0.1 reduce_sum.19
  123.6 0.0 copy-start.1
  123.6 2.7 %broadcast_divide_fusion = f32[16,8,8192]{2,0,1:T(8,128)S(1)} fusion(f32[16,8,8192]{2,0,1:T(8,128)} %get-tuple-element.9, f32[16]{0:T(128)S(1)} %add_sqrt_fusion), kind=kLoop, calls=%fused_computation.25 | loop fusion | flops 1048576 | bytes 8388672 | tf_op jit(solution)/shard_map/div | solution.py:110
  126.3 0.0 copy-done.1
  126.3 4.4 %copy.12 = f32[16,8,8192]{2,1,0:T(8,128)} copy(f32[16,8,8192]{2,0,1:T(8,128)S(1)} %broadcast_divide_fusion) | data formatting | bytes 8388608
  (9 shorter events, 0.2 us)
Async XLA Ops:
  2.0 15.2 %collective-permute-start.1 = (f32[2,1,8192]{2,1,0:T(1,128)S(1)}, f32[2,1,8192]{2,1,0:T(1,128)S(1)}, u32[]{:S(2)}, u32[]{:S(2)}) collective-permute-start(f32[2,1,8192]{2,1,0:T(1,128)S(1)} %pad_maximum_fusion.2), channel_id=1, source_target_pairs={{0,4},{4,8},{8,12},{12,16},{16,20},{20,24},{24,28},{28,32},{32,36}... | collective-permute-start | bytes 196616 | tf_op jit(solution)/shard_map/ppermute | solution.py:11
  11.6 5.0 %copy-start = (f32[4,8,8192]{2,1,0:T(8,128)S(1)}, f32[4,8,8192]{2,1,0:T(8,128)}, u32[]{:S(2)}) copy-start(f32[4,8,8192]{2,1,0:T(8,128)} %param.4) | copy-start | bytes 3145732
  11.6 5.3 %copy-start.2 = (s32[64]{0:T(128)S(1)}, s32[64]{0:T(128)}, u32[]{:S(2)}) copy-start(s32[64]{0:T(128)} %param.5) | copy-start | bytes 772
  11.6 54.7 %all-to-all-start = ((f32[4,16,2,8192]{3,2,1,0:T(2,128)}), f32[4,16,2,8192]{3,2,1,0:T(2,128)}, u32[]{:S(2)}, u32[]{:S(2)}) async-start(f32[4,16,2,8192]{3,2,1,0:T(2,128)} %pad_maximum_fusion), calls=%async_computation | async-start | bytes 8388608 | tf_op jit(solution)/shard_map/all_to_all | solution.py:101
  71.0 15.4 %collective-permute-start = (f32[16,1,8192]{2,0,1:T(8,128)S(1)}, f32[16,1,8192]{2,0,1:T(8,128)S(1)}, u32[]{:S(2)}, u32[]{:S(2)}) collective-permute-start(f32[16,1,8192]{2,0,1:T(8,128)S(1)} %get-tuple-element.12), channel_id=1, source_target_pairs={{4,0},{8,4},{12,8},{16,12},{20,16},{24,20},{28,24},{32,28},{36,32}... | collective-permute-start | bytes 1572872 | tf_op jit(solution)/shard_map/ppermute | solution.py:22
  75.6 17.1 %collective-permute-start.2 = (f32[16,1,8192]{2,0,1:T(8,128)S(1)}, f32[16,1,8192]{2,0,1:T(8,128)S(1)}, u32[]{:S(2)}, u32[]{:S(2)}) collective-permute-start(f32[16,1,8192]{2,0,1:T(8,128)S(1)} %get-tuple-element.13), channel_id=1, source_target_pairs={{0,4},{4,8},{8,12},{12,16},{16,20},{20,24},{24,28},{28,32},{32,36}... | collective-permute-start | bytes 1572872 | tf_op jit(solution)/shard_map/ppermute | solution.py:21
  123.6 2.7 %copy-start.1 = (f32[16]{0:T(128)}, f32[16]{0:T(128)S(1)}, u32[]{:S(2)}) copy-start(f32[16]{0:T(128)S(1)} %add_sqrt_fusion) | copy-start | bytes 196
